TPU v7x, 8 devices: a whole 2x2x1 slice. The times are simulated.
8 devices in a mesh: nodes: 8 (over z, y, x, core).
Axes of the slice: x: 2, y: 2, z: 1, core: 2. Of those that a mesh axis runs over, the one named last changes fastest.
Arguments:
- adjacency: bfloat16 [16384, 16384], P('nodes')
- features: bfloat16 [16384, 100], P('nodes')
- w_one: float32 [100, 128], replicated
- w_two: float32 [128, 47], replicated
- labels: int32 [16384], P('nodes')
- label_mask: int32 [16384], P('nodes')
Outputs:
- output 1: float32 [1], replicated
- output 2: float32 [100, 128], replicated
- output 3: float32 [128, 47], replicated
All inputs are finite; a program needn't handle non-finite values.
Results may differ from a plain program's by a relative error of at most 0.001.
Values are sent between devices in bfloat16 or wider.
A program may use at most 1 GiB of HBM per device.

v0:
```python
import functools

import jax
import jax.numpy as jnp
from jax import lax
from jax.experimental import pallas as pl
from jax.experimental.pallas import tpu as pltpu
from jax.sharding import PartitionSpec as P

MESH = pl.DeviceIdType.MESH
F32, BF16 = jnp.float32, jnp.bfloat16
LANE_CONTRACT = (((1,), (1,)), ((), ()))

ROWS = 2048
TILE = 1024
SLOTS = 6
FLIP = 1280
FEAT = 104
HID = 128
CLS = 48
RED1, RED2 = 112, 64
SUB = TILE // 2


def kernel(adj, feat, w_one_any, w_two_any, label_any, mask_any, out,
           w_one, w_two_t, label, w1t, w2t, w2, ring, flip, xbuf, sbuf, acc1, acc2, hid, s2t, mall, dcls,
           pbuf, rbuf, cbuf, rsbuf, red1, redp1, half1, red2, redp2, half2, fin,
           ring_sem, loc_sem, ag_send, ag_recv, m_send, m_recv,
           d_send, d_recv, rs_send, rs_recv, f_send, f_recv):
    me = lax.axis_index('nodes')
    core, px, py = me % 2, (me // 2) % 2, me // 4

    def device(fy, fx, fc):
        return 4 * ((py + fy) % 2) + 2 * ((px + fx) % 2) + (core + fc) % 2

    partner, xn, yn, diag = device(0, 0, 1), device(0, 1, 0), device(1, 0, 0), device(1, 1, 0)

    def columns(u):
        s, back = u % 16, u // 32
        g, r = (1 - back) * (s // 4) + back * (3 - s // 4), s % 2
        fc = (back + (s // 2) % 2) % 2
        t = (g + 1) // 2
        fx, fy = (t + 1 - r) // 2, (t + r) // 2
        h = (r + (g // 2) * (3 - g)) % 2
        return pl.multiple_of(device(fy, fx, fc) * ROWS + h * TILE, TILE)

    def fetch(u, slot):
        return pltpu.make_async_copy(adj.at[:, pl.ds(columns(u), TILE)], ring.at[slot], ring_sem.at[slot])

    def load(r):
        return fetch(16 * (r // 14) + r % 14 + 2 * (1 - r // 28), r % SLOTS)

    def arrived(slot):
        fetch(0, slot).wait()

    def slot_of(p, s):
        kept = (17 - s) // 16
        return kept * (6 + s) + (1 - kept) * ((4 * (1 - p) + s) % SLOTS)

    def remote(src, dst, ssem, rsem, dev):
        return pltpu.make_async_remote_copy(src_ref=src, dst_ref=dst, send_sem=ssem, recv_sem=rsem,
                                            device_id=(dev,), device_id_type=MESH)

    own = [pltpu.make_async_copy(feat.at[:, pl.ds(h * TILE, TILE)], xbuf.at[h], loc_sem.at[h]) for h in range(2)]
    own.append(pltpu.make_async_copy(mask_any, mall.at[0], loc_sem.at[2]))
    small = [pltpu.make_async_copy(a, b, loc_sem.at[3 + i]) for i, (a, b) in
             enumerate(((w_one_any, w_one), (w_two_any, w_two_t), (label_any, label)))]
    for c in small + own:
        c.start()
    for h in range(2):
        fetch(h, 6 + h).start()
    for r in range(3):
        load(r).start()
    peers = [device(e // 4, (e // 2) % 2, e % 2) for e in range(8)]
    barrier = pltpu.get_barrier_semaphore()
    for e in range(1, 8):
        pl.semaphore_signal(barrier, inc=1, device_id=(peers[e],), device_id_type=MESH)
    for c in small:
        c.wait()
    w1t[...] = jnp.concatenate([w_one[...], jnp.zeros((28, HID), F32)], 0).T[:, :FEAT].astype(BF16)
    wide = jnp.concatenate([w_two_t[...], jnp.zeros((81, HID), F32)], 0)
    w2t[...] = wide[:CLS].astype(BF16)
    w2[...] = wide.T[:, :CLS].astype(BF16)
    acc1[...] = jnp.zeros_like(acc1)
    acc2[...] = jnp.zeros_like(acc2)

    with jax.named_scope('barrier'):
        pl.semaphore_wait(barrier, 7)

    def gather_copy(ph, buf, src, step, dev):
        return remote(src, buf.at[step], ag_send.at[ph, step], ag_recv.at[ph, step], dev)

    def gather_start(ph, buf, srcs):
        for step, h, dev in ((4, 0, xn), (5, 1, yn), (2, 0, partner), (3, 1, partner), (8, 1, xn), (9, 0, yn)):
            gather_copy(ph, buf, srcs[h], step, dev).start()

    def gather_step(ph, buf, s):
        @pl.when(s >= 2)
        def _():
            gather_copy(ph, buf, buf.at[s], s, partner).wait_recv()

        @pl.when((s >= 4) & (s % 4 < 2))
        def _():
            gather_copy(ph, buf, buf.at[s], s + 2, partner).start()

        @pl.when(s == 4)
        def _():
            gather_copy(ph, buf, buf.at[s], 12, yn).start()

        @pl.when(s == 5)
        def _():
            gather_copy(ph, buf, buf.at[s], 13, xn).start()

    def gather_finish(ph, buf):
        for step in range(2, 16):
            gather_copy(ph, buf, buf.at[0], step, partner).wait_send()

    for c in own:
        c.wait()
    gather_start(0, xbuf, [xbuf.at[h] for h in range(2)])
    m_copies = [remote(mask_any, mall.at[e], m_send.at[e], m_recv.at[e], peers[e]) for e in range(1, 8)]
    for c in m_copies:
        c.start()
    for r in range(3, SLOTS):
        load(r).start()

    def flip_rows(slot):
        return ring[slot, :FLIP, :].T

    def pair(acc, rows, x, slots):
        for k in range(2):
            flip[1 - k] = flip_rows(slots[k + 1])
            acc[:rows, FLIP:] += lax.dot_general(x(k), ring[slots[k], FLIP:, :], LANE_CONTRACT, preferred_element_type=F32)
            acc[:rows, :FLIP] += jnp.dot(x(k), flip[k], preferred_element_type=F32)

    arrived(6)
    flip[0] = flip_rows(6)

    def first(i, _):
        s = 2 * i
        slots = [slot_of(0, s), slot_of(0, s + 1), slot_of(0, (s + 2) % 16)]
        with jax.named_scope('wait1'):
            arrived(slots[1])
            pl.when(i < 7)(lambda: arrived(slots[2]))

            @pl.when(i > 1)
            def _():
                for k in range(2):
                    load(s + 2 + k).start()

            for k in range(2):
                gather_step(0, xbuf, s + k)
        pair(acc1, 100, lambda k: xbuf[s + k], slots)
        return 0

    with jax.named_scope('pass1'):
        lax.fori_loop(0, 8, first, 0)
    for h in range(2):
        sbuf[h] = acc1[:, h * TILE:(h + 1) * TILE].astype(BF16)
    gather_start(1, sbuf, [sbuf.at[h] for h in range(2)])

    def second(i, _):
        s = 2 * i
        slots = [slot_of(1, s), slot_of(1, s + 1), slot_of(1, s + 2)]
        with jax.named_scope('wait2'):
            pl.when(i > 0)(lambda: arrived(slots[1]))
            arrived(slots[2])

            @pl.when(i == 0)
            def _():
                for k in range(2):
                    load(18 + k).start()

            @pl.when(i > 1)
            def _():
                for k in range(2):
                    load(s + 16 + k).start()

            for k in range(2):
                gather_step(1, sbuf, s + k)
        for k in range(2):
            hid[:, k * TILE:(k + 1) * TILE] = jnp.maximum(jnp.dot(w1t[...], sbuf[s + k], preferred_element_type=F32), 0.0).astype(BF16)
        pair(acc2, HID, lambda k: hid[:, k * TILE:(k + 1) * TILE], slots)
        return 0

    with jax.named_scope('pass2'):
        lax.fori_loop(0, 8, second, 0)

    ut = hid
    with jax.named_scope('wait_m'):
        for c in m_copies:
            c.wait()
    count = jnp.sum(jnp.sum(mall[...], axis=0).astype(F32))
    classes = lax.broadcasted_iota(jnp.int32, (CLS, 512), 0)

    def heads(i, loss):
        cols = pl.ds(pl.multiple_of(i * 512, 512), 512)
        agg = acc2[:, cols].astype(BF16)
        s2t[:, cols] = agg
        z = jnp.dot(w2t[...], agg, preferred_element_type=F32)
        z = jnp.where(classes < 47, z, -1e30)
        z = z - jnp.max(z, axis=0, keepdims=True)
        logp = z - jnp.log(jnp.sum(jnp.exp(z), axis=0, keepdims=True))
        onehot = (label[:, cols] == classes).astype(F32)
        weight = mall[0, :, cols].astype(F32)
        g2 = (weight * (jnp.exp(logp) - onehot) / count).astype(BF16)
        dcls[:, cols] = g2
        ut[:, cols] = jnp.dot(w2[...], g2, preferred_element_type=F32).astype(BF16)
        return loss + weight * jnp.sum(jnp.where(label[:, cols] == classes, logp, 0.0), axis=0, keepdims=True)

    loss = lax.fori_loop(0, ROWS // 512, heads, jnp.zeros((1, 512), F32))

    to_y = (True, False, False, True, False, True)

    def parts(j, extra):
        if isinstance(j, int) and j < 2:
            return [(pl.ds(0, SUB), j), (pl.ds(SUB, SUB), extra + j)]
        return [(pl.ds(0, TILE), j)]

    def pair_copies(j):
        return [remote(pbuf.at[j % 4, :, cols], rbuf.at[j, :, cols], d_send.at[i], d_recv.at[i], partner)
                for cols, i in parts(j, 8)]

    def link_copies(j):
        return [remote(cbuf.at[j, :, cols], rsbuf.at[j, :, cols], rs_send.at[i], rs_recv.at[i], yn if to_y[j] else xn)
                for cols, i in parts(j, 6)]

    def finalize(j):
        with jax.named_scope('wait_pair'):
            pair_copies(j)[0].wait_recv()
        if j in (4, 5):
            with jax.named_scope('wait_link'):
                for c in link_copies(j - 4):
                    c.wait_recv()
            cbuf[j] = (cbuf[j] + rbuf[j]) + rsbuf[j - 4]
        else:
            cbuf[j] = cbuf[j] + rbuf[j]
        if j < 6:
            link_copies(j)[0].start()

    def sum_copies(red, redp, half, base):
        rows = red.shape[0] // 2
        mine = pl.ds(pl.multiple_of(core * rows, 8), rows)
        links = [remote(half.at[0], half.at[e], f_send.at[base + e], f_recv.at[base + e], dev) for e, dev in ((1, xn), (2, yn), (3, diag))]
        return mine, remote(red, redp, f_send.at[base], f_recv.at[base], partner), links

    mine2, over_chip2, over_chips2 = sum_copies(red2, redp2, half2, 0)
    red2[:CLS, :] = lax.dot_general(dcls[...], s2t[...], LANE_CONTRACT, preferred_element_type=F32)
    red2[CLS:, :] = jnp.broadcast_to(-jnp.sum(loss), (RED2 - CLS, HID))
    over_chip2.start()

    with jax.named_scope('third0'):
        for r in range(29, 32):
            arrived(r % SLOTS)
        for r in (32, 33):
            load(r).start()
        for b in range(2):
            cols = slice(b * SUB, (b + 1) * SUB)
            for q in range(4):
                j = q % 2
                term = jnp.dot(ut[...], ring[(28 + q) % SLOTS, :, cols], preferred_element_type=F32)
                if q < 2:
                    pbuf[j, :, cols] = term
                    pair_copies(j)[b].start()
                else:
                    cbuf[j, :, cols] = term
                if b == 0 and q == 1:
                    over_chip2.wait()
                    half2[0] = red2[mine2, :] + redp2[mine2, :]
                    for c in over_chips2:
                        c.start()
                if b == 1:
                    load(34 + q).start()
                if q >= 2:
                    with jax.named_scope('wait_pair'):
                        pair_copies(j)[b].wait_recv()
                    cbuf[j, :, cols] = cbuf[j, :, cols] + rbuf[j, :, cols]
                    link_copies(j)[b].start()

    def wait_sends(j):
        for c in pair_copies(j):
            c.wait_send()

    def third(k, _):
        for q in range(4):
            r, j, end = 28 + 4 * k + q, 2 * k + q % 2, k // 3
            if q < 2:
                slot = r % SLOTS
                arrived(slot)
            else:
                slot = end * (4 + q) + (1 - end) * (r % SLOTS)
                pl.when(k < 3)(functools.partial(arrived, slot))
            term = jnp.dot(ut[...], ring[slot], preferred_element_type=F32)
            if q < 2:
                pl.when(k == 2)(functools.partial(wait_sends, q))
                pl.when(k == 3)(functools.partial(wait_sends, q + 2))
                pbuf[j % 4] = term
                pair_copies(j)[0].start()
            else:
                cbuf[j] = term
            pl.when(k == 1)(load(r + SLOTS).start)
            if q >= 2:
                for kk in range(1, 4):
                    pl.when(k == kk)(functools.partial(finalize, 2 * kk + q - 2))
        return 0

    with jax.named_scope('pass3'):
        lax.fori_loop(1, 4, third, 0)

    for c in over_chips2:
        c.wait()
    fin2 = pl.ds(pl.multiple_of(RED1 + core * (RED2 // 2), 8), RED2 // 2)
    fin[fin2, :] = (half2[0] + half2[1]) + (half2[2] + half2[3])
    over_pair2 = remote(fin.at[fin2], fin.at[fin2], f_send.at[8], f_recv.at[8], partner)
    over_pair2.start()
    gather_finish(0, xbuf)
    gather_finish(1, sbuf)
    over_pair2.wait()
    fin[RED1 + CLS:, :] = fin[RED1 + CLS:, :] / count
    out2 = pltpu.make_async_copy(fin.at[pl.ds(RED1, RED2)], out.at[pl.ds(RED1, RED2)], loc_sem.at[0])
    out2.start()
    for j in range(4, 8):
        wait_sends(j)

    dw1 = jnp.zeros((FEAT, HID), F32)
    for h, (a, b) in enumerate(((3, 4), (2, 5))):
        z1 = jnp.dot(w1t[...], sbuf[h], preferred_element_type=F32)
        with jax.named_scope('wait_own'):
            link_copies(a)[0].wait_recv()
            link_copies(b)[0].wait_recv()
        g1 = jnp.where(z1 > 0.0, (cbuf[6 + h] + rsbuf[a]) + rsbuf[b], 0.0).astype(BF16)
        dw1 = dw1 + lax.dot_general(sbuf[h], g1, LANE_CONTRACT, preferred_element_type=F32)
    red1[:FEAT, :] = dw1
    red1[FEAT:, :] = jnp.zeros((RED1 - FEAT, HID), F32)

    mine1, over_chip1, over_chips1 = sum_copies(red1, redp1, half1, 4)
    with jax.named_scope('sum_chip'):
        over_chip1.start()
        for j in range(6):
            for c in link_copies(j):
                c.wait_send()
        over_chip1.wait()
    half1[0] = red1[mine1, :] + redp1[mine1, :]
    with jax.named_scope('sum_chips'):
        for c in over_chips1:
            c.start()
        for c in over_chips1:
            c.wait()
    fin[mine1, :] = (half1[0] + half1[1]) + (half1[2] + half1[3])
    over_pair1 = remote(fin.at[mine1], out.at[mine1], f_send.at[9], f_recv.at[9], partner)
    with jax.named_scope('sum_pair'):
        over_pair1.start()
        out1 = pltpu.make_async_copy(fin.at[mine1], out.at[mine1], loc_sem.at[1])
        out1.start()
        for c in (out2, out1, over_pair1):
            c.wait()


def split(total, loss, dw_one, dw_two_t):
    loss[...] = total[RED1 + CLS:RED1 + CLS + 1, :1]
    dw_one[...] = total[:100, :]
    dw_two_t[...] = total[RED1:RED1 + 47, :]


def solution(mesh):
    vmem, anywhere = pl.BlockSpec(memory_space=pltpu.VMEM), pl.BlockSpec(memory_space=pl.ANY)

    def local_step(adj, feat, w_one, w_two, label, mask):
        out = pl.pallas_call(
            kernel,
            out_shape=jax.ShapeDtypeStruct((RED1 + RED2, HID), F32),
            in_specs=[anywhere] * 6,
            out_specs=anywhere,
            scratch_shapes=[
                pltpu.VMEM((100, HID), F32),
                pltpu.VMEM((47, HID), F32),
                pltpu.VMEM((1, ROWS), jnp.int32),
                pltpu.VMEM((HID, FEAT), BF16),
                pltpu.VMEM((CLS, HID), BF16),
                pltpu.VMEM((HID, CLS), BF16),
                pltpu.VMEM((SLOTS + 2, ROWS, TILE), BF16),
                pltpu.VMEM((2, TILE, FLIP), BF16),
                pltpu.VMEM((16, 100, TILE), BF16),
                pltpu.VMEM((16, FEAT, TILE), BF16),
                pltpu.VMEM((FEAT, ROWS), F32),
                pltpu.VMEM((HID, ROWS), F32),
                pltpu.VMEM((HID, ROWS), BF16),
                pltpu.VMEM((HID, ROWS), BF16),
                pltpu.VMEM((8, 1, ROWS), jnp.int32),
                pltpu.VMEM((CLS, ROWS), BF16),
                pltpu.VMEM((4, HID, TILE), F32),
                pltpu.VMEM((8, HID, TILE), F32),
                pltpu.VMEM((8, HID, TILE), F32),
                pltpu.VMEM((6, HID, TILE), F32),
                pltpu.VMEM((RED1, HID), F32),
                pltpu.VMEM((RED1, HID), F32),
                pltpu.VMEM((4, RED1 // 2, HID), F32),
                pltpu.VMEM((RED2, HID), F32),
                pltpu.VMEM((RED2, HID), F32),
                pltpu.VMEM((4, RED2 // 2, HID), F32),
                pltpu.VMEM((RED1 + RED2, HID), F32),
                pltpu.SemaphoreType.DMA((SLOTS + 2,)),
                pltpu.SemaphoreType.DMA((6,)),
                pltpu.SemaphoreType.DMA((2, 16)),
                pltpu.SemaphoreType.DMA((2, 16)),
                pltpu.SemaphoreType.DMA((8,)),
                pltpu.SemaphoreType.DMA((8,)),
                pltpu.SemaphoreType.DMA((10,)),
                pltpu.SemaphoreType.DMA((10,)),
                pltpu.SemaphoreType.DMA((8,)),
                pltpu.SemaphoreType.DMA((8,)),
                pltpu.SemaphoreType.DMA((10,)),
                pltpu.SemaphoreType.DMA((10,)),
            ],
            compiler_params=pltpu.CompilerParams(collective_id=0, has_side_effects=True, vmem_limit_bytes=67043328),
            name='gcn_step',
        )(adj, feat.T, w_one, w_two.T, label.reshape(1, ROWS), mask.reshape(1, ROWS))
        loss, dw_one, dw_two_t = pl.pallas_call(
            split,
            out_shape=[jax.ShapeDtypeStruct(shape, F32) for shape in ((1, 1), (100, HID), (47, HID))],
            in_specs=[vmem],
            out_specs=[vmem] * 3,
            name='split',
        )(out)
        return (loss.reshape(1), dw_one, dw_two_t.T)

    return jax.shard_map(local_step, mesh=mesh, in_specs=(P('nodes', None), P('nodes', None), P(None, None), P(None, None), P('nodes'), P('nodes')), out_specs=(P(None), P(None, None), P(None, None)), check_vma=False)
```

profile of v0, /device:TPU:0, one launch (start us, length us, event | category | flops | bytes accessed | tf_op | source)
XLA Modules:
  0.0 99.6 jit_solution(10688590391437444470)
XLA Ops:
  0.6 97.5 %gcn_step.1.total = f32[176,128]{1,0:T(8,128)} custom-call(bf16[2048,16384]{1,0:T(8,128)(2,1)} %adj.1, bf16[100,2048]{1,0:T(8,128)(2,1)} %bitcast.6, f32[100,128]{1,0:T(8,128)} %w_one_any.1, f32[47,128]{1,0:T(8,128)} %bitcast.7, s32[1,2048]{1,0:T(1,128)} %bitcast.8, s32[1,2048]{1,0:T(1,128)} %bitcast.9), custom_call_target="tpu_custom_call" | custom-call | tf_op jit(solution)/shard_map/gcn_step/pallas_call | solution.py:369
  98.1 1.5 %split.1 = (f32[1,1]{1,0:T(1,128)}, f32[100,128]{1,0:T(8,128)}, f32[47,128]{1,0:T(8,128)}) custom-call(f32[176,128]{1,0:T(8,128)} %gcn_step.1.total), custom_call_target="tpu_custom_call" | custom-call | tf_op jit(solution)/shard_map/split/pallas_call | solution.py:418
where the time goes:
time: 99.8 us; the launch traced here: 99.6 us
  Pallas kernels  99 us (99%)
    pallas_call x1, Pallas kernels, local_step(): pl.pallas_call(kernel, out_shape=jax.ShapeDtypeStruct((RED1 + RED2, HID),...  97.5 us

commit v1 on v0

--- a/solution.py
+++ b/solution.py
@@ -194,7 +194,7 @@
     classes = lax.broadcasted_iota(jnp.int32, (CLS, 512), 0)
 
     def heads(i, loss):
-        cols = pl.ds(pl.multiple_of(i * 512, 512), 512)
+        cols = slice(i * 512, (i + 1) * 512)
         agg = acc2[:, cols].astype(BF16)
         s2t[:, cols] = agg
         z = jnp.dot(w2t[...], agg, preferred_element_type=F32)
@@ -208,7 +208,9 @@
         ut[:, cols] = jnp.dot(w2[...], g2, preferred_element_type=F32).astype(BF16)
         return loss + weight * jnp.sum(jnp.where(label[:, cols] == classes, logp, 0.0), axis=0, keepdims=True)
 
-    loss = lax.fori_loop(0, ROWS // 512, heads, jnp.zeros((1, 512), F32))
+    loss = jnp.zeros((1, 512), F32)
+    for i in range(ROWS // 512):
+        loss = heads(i, loss)
 
     to_y = (True, False, False, True, False, True)
 
@@ -322,13 +324,16 @@
     for j in range(4, 8):
         wait_sends(j)
 
+    z1 = pbuf
+    for h, early in enumerate((3, 2)):
+        z1[h] = jnp.dot(w1t[...], sbuf[h], preferred_element_type=F32)
+        link_copies(early)[0].wait_recv()
+        cbuf[6 + h] = cbuf[6 + h] + rsbuf[early]
     dw1 = jnp.zeros((FEAT, HID), F32)
-    for h, (a, b) in enumerate(((3, 4), (2, 5))):
-        z1 = jnp.dot(w1t[...], sbuf[h], preferred_element_type=F32)
+    for h, late in enumerate((4, 5)):
         with jax.named_scope('wait_own'):
-            link_copies(a)[0].wait_recv()
-            link_copies(b)[0].wait_recv()
-        g1 = jnp.where(z1 > 0.0, (cbuf[6 + h] + rsbuf[a]) + rsbuf[b], 0.0).astype(BF16)
+            link_copies(late)[0].wait_recv()
+        g1 = jnp.where(z1[h] > 0.0, cbuf[6 + h] + rsbuf[late], 0.0).astype(BF16)
         dw1 = dw1 + lax.dot_general(sbuf[h], g1, LANE_CONTRACT, preferred_element_type=F32)
     red1[:FEAT, :] = dw1
     red1[FEAT:, :] = jnp.zeros((RED1 - FEAT, HID), F32)

time: 99.8 us -> 99.1 us (level)
  no operation moved by 1% of the time
where the time goes in v1:
time: 99.1 us; the launch traced here: 99 us
  Pallas kernels  98.4 us (99%)
    pallas_call x1, Pallas kernels, local_step(): pl.pallas_call(kernel, out_shape=jax.ShapeDtypeStruct((RED1 + RED2, HID),...  96.9 us

profile of v1, /device:TPU:0, one launch (start us, length us, event | category | flops | bytes accessed | tf_op | source)
XLA Modules:
  0.0 99.0 jit_solution(10265955827320085481)
XLA Ops:
  0.6 96.9 %gcn_step.1.total = f32[176,128]{1,0:T(8,128)} custom-call(bf16[2048,16384]{1,0:T(8,128)(2,1)} %adj.1, bf16[100,2048]{1,0:T(8,128)(2,1)} %bitcast.6, f32[100,128]{1,0:T(8,128)} %w_one_any.1, f32[47,128]{1,0:T(8,128)} %bitcast.7, s32[1,2048]{1,0:T(1,128)} %bitcast.8, s32[1,2048]{1,0:T(1,128)} %bitcast.9), custom_call_target="tpu_custom_call" | custom-call | tf_op jit(solution)/shard_map/gcn_step/pallas_call | solution.py:374
  97.5 1.5 %split.1 = (f32[1,1]{1,0:T(1,128)}, f32[100,128]{1,0:T(8,128)}, f32[47,128]{1,0:T(8,128)}) custom-call(f32[176,128]{1,0:T(8,128)} %gcn_step.1.total), custom_call_target="tpu_custom_call" | custom-call | tf_op jit(solution)/shard_map/split/pallas_call | solution.py:423
